TPU v7x, 32 devices: a whole 2x2x4 slice. The times are simulated.
32 devices in a mesh: left: 8 (over y, x, core), right: 4 (over z).
Axes of the slice: x: 2, y: 2, z: 4, core: 2. Of those that a mesh axis runs over, the one named last changes fastest.
Arguments:
- signal: float32 [256, 256, 1024], P(None, 'left', 'right'), may hold values from -6 to 6
- symbol_x: float32 [256], replicated, may hold values from 0.3 to 3
- symbol_y: float32 [256], replicated, may hold values from 0.3 to 3
- symbol_z: float32 [1024], replicated, may hold values from 0.3 to 3
Outputs:
- spectrum: float32 [128, 128, 512], P('left', 'right')
All inputs are finite; a program needn't handle non-finite values.
Results may differ from a plain program's by a relative error of at most 0.000096.
Values sent between devices are 32-bit elements; how exact they have to be, the bound alone decides.
A program may use at most 128 MiB of HBM per device.

v0:
```python
import jax
import jax.numpy as jnp
from jax import lax
from jax.sharding import PartitionSpec as P


def transform_table(count):
    rank = jnp.arange(count)
    angle = (
        jnp.pi
        / (4 * count)
        * ((2 * rank[:, None] + 1) * (2 * rank[None, :] + 1) % (8 * count)).astype(jnp.float32)
    )
    return jnp.cos(angle) * (2.0 / count) ** 0.5


def transform_dim(values, dim):
    moved = jnp.tensordot(
        values,
        transform_table(values.shape[dim]),
        axes=([dim], [0]),
        precision=lax.Precision.HIGHEST,
    )
    return jnp.moveaxis(moved, -1, dim)


def body(signal, symbol_x, symbol_y, symbol_z):
    part_values = signal
    part_values = transform_dim(part_values, 0)
    part_values = lax.slice_in_dim(part_values, 0, part_values.shape[0] // 2, axis=0)
    part_values = lax.all_to_all(part_values, "left", split_axis=0, concat_axis=1, tiled=True)
    part_values = transform_dim(part_values, 1)
    pencil_values = lax.slice_in_dim(part_values, 0, part_values.shape[1] // 2, axis=1)
    pencil_values = lax.all_to_all(pencil_values, "right", split_axis=1, concat_axis=2, tiled=True)
    pencil_values = transform_dim(pencil_values, 2)
    pencil_values = lax.slice_in_dim(pencil_values, 0, pencil_values.shape[2] // 2, axis=2)
    share_x = pencil_values.shape[0]
    part_x = lax.dynamic_slice_in_dim(symbol_x, lax.axis_index("left") * share_x, share_x)
    share_y = pencil_values.shape[1]
    part_y = lax.dynamic_slice_in_dim(symbol_y, lax.axis_index("right") * share_y, share_y)
    symbol = (
        part_x[:, None, None]
        + part_y[None, :, None]
        + symbol_z[: pencil_values.shape[2]][None, None, :]
    )
    pencil_values = pencil_values * ((1.0 - 0.2 * symbol) / (1.0 + 0.2 * symbol))
    return pencil_values


def solution(mesh):
    in_specs = (P(None, "left", "right"), P(), P(), P())
    out_specs = P("left", "right", None)
    return jax.shard_map(body, mesh=mesh, in_specs=in_specs, out_specs=out_specs, check_vma=False)
```

profile of v0, /device:TPU:0, one launch (start us, length us, event | category | flops | bytes accessed | tf_op | source)
XLA Modules:
  0.0 144.7 jit_solution(14525953596823520953)
XLA Ops:
  0.0 1.0 fusion.17
  1.0 13.0 %fusion = f32[128,32,256]{2,0,1:T(8,128)S(1)} fusion(f32[256,32,256]{2,1,0:T(8,128)} %param.4, f32[256,256,1]{1,0,2:T(8,128)S(1)} %fusion.17), kind=kOutput, calls=%fused_computation | convolution fusion | flops 3221225472 | bytes 12713984 | tf_op jit(solution)/shard_map/dot_general | solution.py:18
  14.1 2.4 %copy.24 = f32[128,32,256]{2,1,0:T(8,128)S(1)} copy(f32[128,32,256]{2,0,1:T(8,128)S(1)} %fusion) | data formatting | bytes 8388608 | tf_op jit(solution)/shard_map/slice | solution.py:30
  16.5 54.0 %all_to_all.36 = f32[128,32,256]{2,1,0:T(8,128)S(1)} all-to-all(f32[128,32,256]{2,1,0:T(8,128)S(1)} %copy.24), channel_id=1, replica_groups=mesh['left'=8,'right'=4] {'left'}, dimensions={0} | all-to-all | bytes 8388608 | tf_op jit(solution)/shard_map/all_to_all | solution.py:31
  70.5 0.6 copy.25
  71.1 7.6 %convolution_bitcast_fusion = f32[16,256,256]{1,2,0:T(8,128)S(1)} fusion(f32[16,256,256]{2,1,0:T(8,128)S(1)} %bitcast.17, s32[256]{0:T(256)S(1)} %multiply_add_fusion.1), kind=kOutput, calls=%fused_computation.13 | convolution fusion | flops 3222208512 | bytes 8389632 | tf_op jit(solution)/shard_map/dot_general | solution.py:18
  78.7 0.2 slice.19
  78.9 0.0 copy-start
  78.9 0.0 copy-start.1
  78.9 2.1 %copy.27 = f32[16,128,256]{2,0,1:T(8,128)} copy(f32[16,128,256]{1,2,0:T(8,128)S(1)} %slice.19) | data formatting | bytes 4194304 | tf_op jit(solution)/shard_map/slice | solution.py:33
  81.0 4.9 %all-to-all-start.1 = ((f32[16,128,256]{2,0,1:T(8,128)}), f32[16,128,256]{2,0,1:T(8,128)S(1)}, u32[]{:S(2)}, u32[]{:S(2)}) async-start(f32[16,128,256]{2,0,1:T(8,128)} %copy.27), calls=%async_computation.1 | async-start | bytes 4194304 | tf_op jit(solution)/shard_map/all_to_all | solution.py:34
  85.8 0.0 copy-done
  85.8 0.1 dynamic_slice.7
  85.9 0.0 copy-done.1
  85.9 0.1 dynamic_slice.6
  86.0 0.1 broadcast_add_fusion
  86.1 16.7 %fusion.6 = f32[1024,1024,1]{1,0,2:T(8,128)} fusion(s32[1024]{0:T(1024)S(1)} %multiply_add_fusion), kind=kLoop, calls=%fused_computation.11 | loop fusion | flops 15728640 | bytes 4198400 | tf_op jit(solution)/shard_map/mul | solution.py:14
  102.8 30.7 %all-to-all-done.1 = f32[16,128,256]{2,0,1:T(8,128)S(1)} async-done(((f32[16,128,256]{2,0,1:T(8,128)}), f32[16,128,256]{2,0,1:T(8,128)S(1)}, u32[]{:S(2)}, u32[]{:S(2)}) %all-to-all-start.1) | async-done | bytes 2097184 | tf_op jit(solution)/shard_map/all_to_all | solution.py:34
  133.5 0.0 slice-start
  133.5 2.7 %copy.29 = f32[16,32,4,256]{3,2,1,0:T(4,128)} copy(f32[16,32,4,256]{3,0,1,2:T(8,128)S(1)} %bitcast.19) | data formatting | bytes 4194304 | tf_op jit(solution)/shard_map/all_to_all | solution.py:34
  136.2 2.3 %all_to_all.33 = f32[16,32,1024]{2,1,0:T(8,128)S(1)} reshape(f32[16,32,4,256]{3,2,1,0:T(4,128)} %copy.29) | data formatting | bytes 4194304 | tf_op jit(solution)/shard_map/all_to_all | solution.py:34
  138.5 0.0 slice-done
  138.5 6.2 %fusion.10 = f32[16,32,512]{2,1,0:T(8,128)} fusion(f32[16,32,1024]{2,1,0:T(8,128)S(1)} %all_to_all.33, f32[1024,1024,1]{1,0,2:T(8,128)} %fusion.6, f32[512]{0:T(512)S(1)} %slice-done, f32[16,32]{1,0:T(8,128)S(1)} %broadcast_add_fusion), kind=kOutput, calls=%fused_computation.16 | convolution fusion | flops 3222798336 | bytes 5246976 | tf_op jit(solution)/shard_map/dot_general | solution.py:18
  (2 shorter events, 0.0 us)
Async XLA Ops:
  78.9 7.0 %copy-start = (f32[256]{0:T(256)S(1)}, f32[256]{0:T(256)}, u32[]{:S(2)}) copy-start(f32[256]{0:T(256)} %param.6) | copy-start | bytes 3076
  78.9 7.0 %copy-start.1 = (f32[256]{0:T(256)S(1)}, f32[256]{0:T(256)}, u32[]{:S(2)}) copy-start(f32[256]{0:T(256)} %param.5) | copy-start | bytes 3076
  81.0 52.5 %all-to-all-start.1 = ((f32[16,128,256]{2,0,1:T(8,128)}), f32[16,128,256]{2,0,1:T(8,128)S(1)}, u32[]{:S(2)}, u32[]{:S(2)}) async-start(f32[16,128,256]{2,0,1:T(8,128)} %copy.27), calls=%async_computation.1 | async-start | bytes 4194304 | tf_op jit(solution)/shard_map/all_to_all | solution.py:34
  133.5 5.0 %slice-start = ((f32[1024]{0:T(1024)}), f32[512]{0:T(512)S(1)}, s32[]{:S(2)}) async-start(f32[1024]{0:T(1024)} %param.7), calls=%async_computation.2 | async-start | bytes 4096 | tf_op jit(solution)/shard_map/slice | solution.py:44
where the time goes:
time: 145 us
  blocking collectives  54 us (37%)
  waiting for transfers between devices  30.7 us (21%)
  matrix products  26.8 us (18%)
  other arithmetic  17.8 us (12%)
  local copies, waits for them, and re-layouts  10.4 us (7%)
  starting transfers between devices  4.87 us (3%)
    all_to_all x1, blocking collectives, body(): lax.all_to_all(part_values, 'left', split_axis=0, concat_axis=1, tiled=True)  54 us
    all_to_all x1, waiting for transfers between devices, body(): lax.all_to_all(pencil_values, 'right', split_axis=1, concat_axis=2, tiled...  30.7 us
    dot_general x3, matrix products, transform_dim(): jnp.tensordot(values, transform_table(values.shape[dim]), axes=([dim], [0...  26.8 us
    mul x2, other arithmetic, transform_table(): return jnp.cos(angle) * (2.0 / count) ** 0.5  17.7 us
    all_to_all x2, local copies, waits for them, and re-layouts, body(): lax.all_to_all(pencil_values, 'right', split_axis=1, concat_axis=2, tiled...  5 us
    all_to_all x1, starting transfers between devices, body(): lax.all_to_all(pencil_values, 'right', split_axis=1, concat_axis=2, tiled...  4.87 us
  transfers between devices with their start and end apart: 1, of which 1 were waited for; matrix products, arithmetic and copies ran while one was open for 12% of the time, Pallas kernels for 0%

commit v1 on v0

--- a/solution.py
+++ b/solution.py
@@ -31,7 +31,12 @@
     part_values = lax.all_to_all(part_values, "left", split_axis=0, concat_axis=1, tiled=True)
     part_values = transform_dim(part_values, 1)
     pencil_values = lax.slice_in_dim(part_values, 0, part_values.shape[1] // 2, axis=1)
-    pencil_values = lax.all_to_all(pencil_values, "right", split_axis=1, concat_axis=2, tiled=True)
+    pencil_values = jnp.concatenate(
+        lax.all_to_all(
+            jnp.stack(jnp.split(pencil_values, lax.axis_size("right"), axis=1)), "right", 0, 0
+        ),
+        axis=2,
+    )
     pencil_values = transform_dim(pencil_values, 2)
     pencil_values = lax.slice_in_dim(pencil_values, 0, pencil_values.shape[2] // 2, axis=2)
     share_x = pencil_values.shape[0]

time: 145 us -> 137 us (0.945)
  local copies, waits for them, and re-layouts: 10.4 us -> 5.48 us
  matrix products: 26.8 us -> 22.6 us
  other arithmetic: 17.8 us -> 19.3 us
    all_to_all x2 -> x0, local copies, waits for them, and re-layouts: 5 us -> none  [body(): lax.all_to_all(pencil_values, 'right', split_axis=1, concat_axis=2, tiled...]
    dot_general x3, matrix products: 26.8 us -> 22.6 us  [transform_dim(): jnp.tensordot(values, transform_table(values.shape[dim]), axes=([dim], [0...]
    slice x2 -> x0, local copies, waits for them, and re-layouts: 2.24 us -> none  [body(): lax.slice_in_dim(part_values, 0, part_values.shape[1] // 2, axis=1)]
    unnamed x4 -> x6, local copies, waits for them, and re-layouts: 0.01 us -> 1.88 us
    another operation x0 -> x1, other arithmetic: none -> 1.47 us  [body(): jnp.stack(jnp.split(pencil_values, lax.axis_size('right'), axis=1))]
where the time goes in v1:
time: 137 us
  blocking collectives  54 us (39%)
  waiting for transfers between devices  30.7 us (22%)
  matrix products  22.6 us (16%)
  other arithmetic  19.3 us (14%)
  local copies, waits for them, and re-layouts  5.48 us (4%)
  starting transfers between devices  4.87 us (4%)
    all_to_all x1, blocking collectives, body(): lax.all_to_all(part_values, 'left', split_axis=0, concat_axis=1, tiled=True)  54 us
    all_to_all x1, waiting for transfers between devices, body(): lax.all_to_all(jnp.stack(jnp.split(pencil_values, lax.axis_size('right'),...  30.7 us
    dot_general x3, matrix products, transform_dim(): jnp.tensordot(values, transform_table(values.shape[dim]), axes=([dim], [0...  22.6 us
    mul x2, other arithmetic, transform_table(): return jnp.cos(angle) * (2.0 / count) ** 0.5  17.7 us
    all_to_all x1, starting transfers between devices, body(): lax.all_to_all(jnp.stack(jnp.split(pencil_values, lax.axis_size('right'),...  4.87 us
  transfers between devices with their start and end apart: 1, of which 1 were waited for; matrix products, arithmetic and copies ran while one was open for 12% of the time, Pallas kernels for 0%

profile of v1, /device:TPU:0, one launch (start us, length us, event | category | flops | bytes accessed | tf_op | source)
XLA Modules:
  0.0 137.0 jit_solution(2609912275605393516)
XLA Ops:
  0.0 1.0 fusion.17
  1.0 13.0 %fusion = f32[128,32,256]{2,0,1:T(8,128)S(1)} fusion(f32[256,32,256]{2,1,0:T(8,128)} %param.4, f32[256,256,1]{0,1,2:T(8,128)S(1)} %fusion.17), kind=kOutput, calls=%fused_computation | convolution fusion | flops 3221225472 | bytes 12713984 | tf_op jit(solution)/shard_map/dot_general | solution.py:18
  14.0 2.4 %copy.11 = f32[128,32,256]{2,1,0:T(8,128)S(1)} copy(f32[128,32,256]{2,0,1:T(8,128)S(1)} %fusion) | data formatting | bytes 8388608 | tf_op jit(solution)/shard_map/slice | solution.py:30
  16.5 54.0 %all_to_all.23 = f32[128,32,256]{2,1,0:T(8,128)S(1)} all-to-all(f32[128,32,256]{2,1,0:T(8,128)S(1)} %copy.11), channel_id=1, replica_groups=mesh['left'=8,'right'=4] {'left'}, dimensions={0} | all-to-all | bytes 8388608 | tf_op jit(solution)/shard_map/all_to_all | solution.py:31
  70.5 0.6 copy.12
  71.1 5.0 %convolution_bitcast_fusion = f32[16,256,256]{2,1,0:T(8,128)S(1)} fusion(f32[16,256,256]{2,1,0:T(8,128)S(1)} %bitcast.24, s32[256]{0:T(256)S(1)} %multiply_add_fusion.1), kind=kOutput, calls=%fused_computation.13 | convolution fusion | flops 3222208512 | bytes 8389632 | tf_op jit(solution)/shard_map/dot_general | solution.py:18
  76.1 0.1 slice_bitcast_fusion.3
  76.2 0.0 copy-start.1
  76.3 0.0 copy-start.2
  76.3 1.5 %pad_maximum_fusion = f32[4,16,32,256]{3,2,1,0:T(8,128)} fusion(f32[1,16,32,256]{3,2,1,0:T(8,128)S(1)} %get-tuple-element.6, f32[1,16,32,256]{3,2,1,0:T(8,128)S(1)} %get-tuple-element.7, f32[1,16,32,256]{3,2,1,0:T(8,128)S(1)} %get-tuple-element.8, f32[1,16,32,256]{3,2,1,0:T(8,128)S(1)} %get-tuple-element.5), kind=kLoop, calls=%fused_computation.16 | loop fusion | flops 1572864 | bytes 4194304 | tf_op jit(solution)/shard_map/stack | solution.py:36
  77.7 4.9 %all-to-all-start.1 = ((f32[4,16,32,256]{3,2,1,0:T(8,128)}), f32[4,16,32,256]{3,2,1,0:T(8,128)S(1)}, u32[]{:S(2)}, u32[]{:S(2)}) async-start(f32[4,16,32,256]{3,2,1,0:T(8,128)} %pad_maximum_fusion), calls=%async_computation.1 | async-start | bytes 4194304 | tf_op jit(solution)/shard_map/all_to_all | solution.py:35
  82.6 0.0 copy-done.1
  82.6 0.1 dynamic_slice.6
  82.7 0.0 copy-done.2
  82.7 0.1 dynamic_slice.7
  82.8 0.1 broadcast_add_fusion
  82.8 0.0 slice-start
  82.8 16.7 %fusion.6 = f32[1024,1024,1]{1,0,2:T(8,128)} fusion(s32[1024]{0:T(1024)S(1)} %multiply_add_fusion), kind=kLoop, calls=%fused_computation.11 | loop fusion | flops 15728640 | bytes 4198400 | tf_op jit(solution)/shard_map/mul | solution.py:14
  99.5 30.7 %all-to-all-done.1 = f32[4,16,32,256]{3,2,1,0:T(8,128)S(1)} async-done(((f32[4,16,32,256]{3,2,1,0:T(8,128)}), f32[4,16,32,256]{3,2,1,0:T(8,128)S(1)}, u32[]{:S(2)}, u32[]{:S(2)}) %all-to-all-start.1) | async-done | bytes 2097184 | tf_op jit(solution)/shard_map/all_to_all | solution.py:35
  130.3 0.0 copy-start
  130.3 0.3 copy.14
  130.6 0.0 slice-done
  130.6 1.9 %copy-done = f32[1024,1024,1]{1,0,2:T(8,128)S(1)} copy-done((f32[1024,1024,1]{1,0,2:T(8,128)S(1)}, f32[1024,1024,1]{1,0,2:T(8,128)}, u32[]{:S(2)}) %copy-start) | copy-done | bytes 4194328
  132.4 4.6 %fusion.10 = f32[16,32,512]{2,1,0:T(8,128)} fusion(f32[16,32,1024]{2,1,0:T(8,128)S(1)} %bitcast.27, f32[1024,1024,1]{1,0,2:T(8,128)S(1)} %copy-done, f32[512]{0:T(512)S(1)} %slice-done, f32[16,32]{1,0:T(8,128)S(1)} %broadcast_add_fusion), kind=kOutput, calls=%fused_computation.17 | convolution fusion | flops 3222798336 | bytes 5253120 | tf_op jit(solution)/shard_map/dot_general | solution.py:18
  (2 shorter events, 0.0 us)
Async XLA Ops:
  76.2 6.4 %copy-start.1 = (f32[256]{0:T(256)S(1)}, f32[256]{0:T(256)}, u32[]{:S(2)}) copy-start(f32[256]{0:T(256)} %param.5) | copy-start | bytes 3076
  76.3 6.4 %copy-start.2 = (f32[256]{0:T(256)S(1)}, f32[256]{0:T(256)}, u32[]{:S(2)}) copy-start(f32[256]{0:T(256)} %param.6) | copy-start | bytes 3076
  77.7 52.5 %all-to-all-start.1 = ((f32[4,16,32,256]{3,2,1,0:T(8,128)}), f32[4,16,32,256]{3,2,1,0:T(8,128)S(1)}, u32[]{:S(2)}, u32[]{:S(2)}) async-start(f32[4,16,32,256]{3,2,1,0:T(8,128)} %pad_maximum_fusion), calls=%async_computation.1 | async-start | bytes 4194304 | tf_op jit(solution)/shard_map/all_to_all | solution.py:35
  82.8 47.7 %slice-start = ((f32[1024]{0:T(1024)}), f32[512]{0:T(512)S(1)}, s32[]{:S(2)}) async-start(f32[1024]{0:T(1024)} %param.7), calls=%async_computation.2 | async-start | bytes 4096 | tf_op jit(solution)/shard_map/slice | solution.py:49
  130.3 2.2 %copy-start = (f32[1024,1024,1]{1,0,2:T(8,128)S(1)}, f32[1024,1024,1]{1,0,2:T(8,128)}, u32[]{:S(2)}) copy-start(f32[1024,1024,1]{1,0,2:T(8,128)} %fusion.6) | copy-start | bytes 12582916
